TPU v7x, 256 devices: a whole 4x4x8 slice. The times are simulated.
256 devices in a mesh: shell: 16 (over x, z_lo, core), sky: 16 (over y, z_hi).
Axes of the slice: x: 4, y: 4, z: 8 (z_hi: 4, z_lo: 2; z = z_hi * 2 + z_lo), core: 2. Of those that a mesh axis runs over, the one named last changes fastest.
Arguments:
- coords: int32 [3, 16, 16, 512], P(None, 'shell', 'sky'), may hold values from 0 to 4095, as said below
- weights: bfloat16 [16, 16, 512], P('shell', 'sky'), may hold values from 0.5 to 2
- live: int32 [16, 16], P('shell', 'sky'), may hold values from 128 to 512, as said below
Outputs:
- jackknife: float32 [16, 128, 600], P('shell', 'sky')
Inputs may be any that keep to these rules, and one draw needn't show every extreme that they name: On device (a, b), coords[0] lies in [a * 256, (a+1) * 256), coords[1] in [b * 256, (b+1) * 256), coords[2] in [0, 1024). `live`: live slots are the first ones of a device; some device is full in every draw.
All inputs are finite; a program needn't handle non-finite values.
Results may differ from a plain program's by a relative error of at most 0.0003.
Values sent between devices are 32-bit elements; how exact they have to be, the bound alone decides.
A program may use at most 64 MiB of HBM per device.

v0:
```python
import functools, math
import jax, jax.numpy as jnp
from jax import lax
from jax.experimental import pallas as pl
from jax.experimental.pallas import tpu as pltpu
from jax.sharding import PartitionSpec as P

PART_DEV = 512
SIDE_CELLS = 256
SPAN_CELLS = 1024
SUBREGIONS = 8
S_BINS = 30
MU_BINS = 20
REACH = 199
EARLY = 3
GROUPS = 24
STEP = 16
ROWS = PART_DEV // STEP
DUMMY = 9 * ROWS
TILES = 4
DIRS = tuple((da, db) for da in (-1, 0, 1) for db in (-1, 0, 1) if (da, db) != (0, 0))
ORDER = (0, 2, 5, 7, 3, 4, 1, 6)
MESH = pl.DeviceIdType.MESH
F32 = jnp.float32
BF16 = jnp.bfloat16


def send_kernel(coords_hbm, weight_hbm, live_hbm, table_ref, rows_ref, own_ref, coords_ref, weight_ref, live_ref, lists_ref, got_ref, load_sem, send_sem, recv_sem):
    shell, sky = lax.axis_index("shell"), lax.axis_index("sky")
    shells, skies = lax.axis_size("shell"), lax.axis_size("sky")
    barrier = pltpu.get_barrier_semaphore()
    loads = [
        pltpu.make_async_copy(src, dst, load_sem.at[k])
        for k, (src, dst) in enumerate(((coords_hbm, coords_ref), (weight_hbm, weight_ref), (live_hbm, live_ref)))
    ]
    for load in loads:
        load.start()

    def present(da, db):
        a, b = shell + da, sky + db
        return (a >= 0) & (a < shells) & (b >= 0) & (b < skies)

    for da, db in DIRS:

        @pl.when(present(da, db))
        def _():
            pl.semaphore_signal(barrier, inc=1, device_id=(shell + da, sky + db), device_id_type=MESH)

    for d, (da, db) in enumerate(DIRS):

        @pl.when(jnp.logical_not(present(da, db)))
        def _():
            got_ref[d] = jnp.zeros((4, PART_DEV), F32)

    def copy(d):
        da, db = DIRS[d]
        return pltpu.make_async_remote_copy(
            src_ref=lists_ref.at[d],
            dst_ref=got_ref.at[7 - d],
            send_sem=send_sem.at[d],
            recv_sem=recv_sem.at[7 - d],
            device_id=(shell + da, sky + db),
            device_id_type=MESH,
        )

    def body(acc0, acc1, acc2, acc3, tall0, tall1):
        for acc in (acc0, acc1, acc2, acc3, tall0, tall1):
            pltpu.matmul_pop(acc)
        for load in loads:
            load.wait()
        n = PART_DEV
        x = (coords_ref[0, 0] & (SIDE_CELLS - 1)).astype(F32)
        y = (coords_ref[1, 0] & (SIDE_CELLS - 1)).astype(F32)
        zi = coords_ref[2, 0]
        region = zi >> 7
        z_high = region.astype(F32)
        z_low = (zi & 127).astype(F32)
        slot = lax.broadcasted_iota(jnp.int32, (1, n), 1)
        alive = slot < live_ref[...]
        w = jnp.where(alive, weight_ref[0].astype(F32), 0.0)
        key = (jnp.where(alive, zi * n, SPAN_CELLS * n) + slot).astype(F32)
        key_column = jnp.transpose(jnp.broadcast_to(key, (128, n)))[:, 0:1]
        before = jnp.where(key_column < key, 1.0, 0.0).astype(BF16)
        valid = []
        for da, db in DIRS:
            ok = alive
            if da > 0:
                ok = ok & (x >= SIDE_CELLS - REACH)
            if da < 0:
                ok = ok & (x <= REACH - 1)
            if db > 0:
                ok = ok & (y >= SIDE_CELLS - REACH)
            if db < 0:
                ok = ok & (y <= REACH - 1)
            valid.append(ok)
        valid.append(alive)
        ones = [jnp.where(ok, 1.0, 0.0) for ok in valid]
        flags = jnp.concatenate(ones + [jnp.zeros((7, n), F32)], axis=0).astype(BF16)
        for half in range(2):
            rows = slice(256 * half, 256 * half + 256)
            pltpu.matmul_push_rhs(before[rows, 0:256], staging_register=0, mxu_index=0)
            pltpu.matmul_acc_lhs(acc0, flags[:, rows], load_staged_rhs=0)
            pltpu.matmul_push_rhs(before[rows, 256:512], staging_register=0, mxu_index=1)
            pltpu.matmul_acc_lhs(acc1, flags[:, rows], load_staged_rhs=0)
        rank = jnp.concatenate([pltpu.matmul_pop(acc0), pltpu.matmul_pop(acc1)], axis=1)
        attrs = jnp.concatenate([x, y, z_high, z_low, w, jnp.zeros((11, n), F32)], axis=0).astype(BF16)
        place = lax.broadcasted_iota(jnp.int32, (256, n), 0).astype(F32).astype(BF16)
        one, zero = jnp.ones((256, n), BF16), jnp.zeros((256, n), BF16)
        accs = ((acc0, acc1), (acc2, acc3))
        beside_shell = 1 + (shell > 0).astype(jnp.int32) + (shell < shells - 1).astype(jnp.int32)
        beside_sky = 1 + (sky > 0).astype(jnp.int32) + (sky < skies - 1).astype(jnp.int32)

        def build(d, slot):
            target = jnp.where(valid[d], rank[d : d + 1, :], -1.0)
            pair = accs[slot % 2]
            for mxu in range(2):
                near = jnp.broadcast_to((target - 256.0 * mxu).astype(BF16), (256, n))
                hot = jnp.where(place == near, one, zero)
                for half in range(2):
                    cols = slice(256 * half, 256 * half + 256)
                    pltpu.matmul_push_rhs(hot[:, cols], staging_register=0, mxu_index=mxu, transpose=True)
                    pltpu.matmul_acc_lhs(pair[mxu], attrs[:, cols], load_staged_rhs=0)
            da, db = DIRS[d] if d < 8 else (0, 0)
            for mxu in range(2):
                got = pltpu.matmul_pop(pair[mxu])
                lanes = slice(256 * mxu, 256 * mxu + 256)
                lists_ref[d, 0:1, lanes] = got[0:1] - float(SIDE_CELLS * da)
                lists_ref[d, 1:2, lanes] = got[1:2] - float(SIDE_CELLS * db)
                lists_ref[d, 2:3, lanes] = got[2:3] * 128.0 + got[3:4]
                lists_ref[d, 3:4, lanes] = got[4:5]

        for slot, d in enumerate(ORDER):
            build(d, slot)
        pl.semaphore_wait(barrier, beside_shell * beside_sky - 1)
        for d in ORDER:

            @pl.when(present(*DIRS[d]))
            def _():
                copy(d).start()

        build(8, 0)
        shift = jnp.zeros((1, n), F32)
        first = jnp.zeros((1, 1), F32)
        group = jnp.zeros((1, 1), F32)
        starts = []
        for r in range(SUBREGIONS):
            here = alive & (region == r)
            starts.append(group)
            shift = jnp.where(here, 32.0 * group - first, shift)
            count = jnp.sum(jnp.where(here, 1.0, 0.0), axis=1, keepdims=True)
            first = first + count
            group = group + jnp.floor((count + 31.0) * (1.0 / 32.0))
        starts = starts + [group]
        lane_row = lax.broadcasted_iota(jnp.int32, (1, 128), 1)
        begin, end = jnp.zeros((1, 128), F32), jnp.zeros((1, 128), F32)
        for r in range(SUBREGIONS):
            begin = jnp.where(lane_row == r, starts[r], begin)
            end = jnp.where(lane_row == r, starts[r + 1], end)
        target = jnp.where(alive, rank[8:9, :] + shift, -1.0)
        wide = lax.broadcasted_iota(jnp.int32, (GROUPS * 32, 1), 0).astype(F32)
        hot = jnp.where(wide == target, 1.0, 0.0).astype(BF16)
        rhs = jnp.concatenate([attrs, jnp.zeros((240, n), BF16)], axis=0)
        half_rows = GROUPS * 16
        for half in range(2):
            cols = slice(256 * half, 256 * half + 256)
            for mxu, acc in ((0, tall0), (1, tall1)):
                pltpu.matmul_push_rhs(rhs[:, cols], staging_register=0, mxu_index=mxu, transpose=True)
                pltpu.matmul_acc_lhs(acc, hot[half_rows * mxu : half_rows * mxu + half_rows, cols], load_staged_rhs=0)
        quarter = lax.broadcasted_iota(jnp.int32, (8, 128), 1) // 32
        for mxu, acc in ((0, tall0), (1, tall1)):
            got = pltpu.matmul_pop(acc)[:, 0:128]
            for g in range(GROUPS // 2):
                parts = []
                for q in range(4):
                    block = got[32 * g + 8 * q : 32 * g + 8 * q + 8]
                    deep = block[:, 2:3] * 128.0 + block[:, 3:4]
                    parts.append([jnp.broadcast_to(v, (8, 128)) for v in (block[:, 0:1], block[:, 1:2], deep, block[:, 4:5])])
                for k in range(4):
                    value = parts[0][k]
                    for q in range(1, 4):
                        value = jnp.where(quarter == q, parts[q][k], value)
                    own_ref[k, mxu * (GROUPS // 2) + g] = value

        zs, ws = own_ref[2], own_ref[3]
        z_min = jnp.min(jnp.min(jnp.where(ws > 0.0, zs, 1e6), axis=1), axis=1, keepdims=True)
        z_max = jnp.max(jnp.max(jnp.where(ws > 0.0, zs, -1e6), axis=1), axis=1, keepdims=True)
        lane = lax.broadcasted_iota(jnp.int32, (GROUPS, 128), 1)
        chunk = lane.astype(F32) * 2.0
        even = jnp.full((GROUPS, 128), float(DUMMY), F32)
        odd = even
        total = jnp.zeros((GROUPS, 1), F32)
        lane8 = lax.broadcasted_iota(jnp.int32, (8, 128), 1)
        rows_ref[DUMMY] = jnp.zeros((8, 128), F32)
        for d in (8, 1, 6, 3, 4, 0, 2, 5, 7):
            if d < 8:

                @pl.when(present(*DIRS[d]))
                def _():
                    copy(7 - d).wait_recv()

            src = lists_ref.at[8] if d == 8 else got_ref.at[d]
            z_row = jnp.where(src[3:4, :] > 0.0, src[2:3, :], 2e6)
            low = jnp.sum(jnp.where(z_row < z_min - float(REACH), 1.0, 0.0), axis=1, keepdims=True)
            high = jnp.sum(jnp.where(z_row <= z_max + float(REACH), 1.0, 0.0), axis=1, keepdims=True)
            first = jnp.floor(low * (1.0 / STEP))
            count = jnp.where(high > low, jnp.floor((high - STEP * first + 31.0) * (1.0 / 32.0)), 0.0)
            at = chunk - total
            even = jnp.where((at >= 0.0) & (at < count), at * 2.0 + (first + float(ROWS * d)), even)
            at = at + 1.0
            odd = jnp.where((at >= 0.0) & (at < count), at * 2.0 + (first + float(ROWS * d)), odd)
            total = total + count
            parts = []
            for t in range(4):
                block = src[:, 128 * t : 128 * t + 128]
                block = jnp.concatenate([block, block], axis=0)
                for k in range(4):
                    part = block if k == 0 else pltpu.roll(block, 128 - 32 * k, 1)
                    part = jnp.where(lane8 < 32, part, pltpu.roll(part, 32, 1))
                    part = jnp.where(lane8 < 64, part, pltpu.roll(part, 64, 1))
                    parts.append(part)
            turned = [pltpu.roll(part, 16, 1) for part in parts] + [jnp.zeros((8, 128), F32)]
            for k in range(16):
                rows_ref[ROWS * d + 2 * k] = parts[k]
                rows_ref[ROWS * d + 2 * k + 1] = jnp.where((lane8 & 31) < 16, turned[k], turned[k + 1])
        units = jnp.floor((total + 1.0) * 0.5)
        name = lax.broadcasted_iota(jnp.int32, (GROUPS, 128), 0).astype(F32)
        number = jnp.sum(jnp.where((name >= begin) & (name < end), units, 0.0), axis=0, keepdims=True)
        turns = jnp.floor((number + 3.0) * 0.25)
        extra = 4.0 * turns - number
        units = units + jnp.sum(jnp.where(name == end - 1.0, extra, 0.0), axis=1, keepdims=True)
        skip = 4.0 * EARLY
        other = lane.astype(F32)
        units_row = jnp.sum(jnp.where(name == other, units, 0.0), axis=0, keepdims=True)
        origin = jnp.zeros((GROUPS, 1), F32)
        for r in range(SUBREGIONS):
            origin = jnp.where(name[:, 0:1] >= starts[r], starts[r], origin)
        passed = jnp.sum(jnp.where((other < name) & (other >= origin), units_row, 0.0), axis=1, keepdims=True)
        hit = (name >= begin) & (name < end) & (passed <= skip) & (skip < passed + units)
        found = jnp.sum(jnp.where(hit, 1.0, 0.0), axis=0, keepdims=True)
        start_g = jnp.sum(jnp.where(hit, name, 0.0), axis=0, keepdims=True)
        start_b = jnp.sum(jnp.where(hit, skip - passed, 0.0), axis=0, keepdims=True)
        real = lane_row < SUBREGIONS
        late = jnp.where(real, jnp.maximum(turns - EARLY, 1.0), float(1 << 18))
        start_g = jnp.where(found > 0.0, start_g, float(GROUPS))
        open_g = jnp.where(real & (begin < end), begin, float(GROUPS))
        table = jnp.where(lane == 127, units, even + 512.0 * odd)
        idle = jnp.where(lane_row == 127, float(1 << 20), float(DUMMY * 513))
        tail = [idle, late, start_g, start_b, open_g, end, jnp.zeros((2, 128), F32)]
        table_ref[...] = jnp.concatenate([table] + tail, axis=0).astype(jnp.int32)
        for d, (da, db) in enumerate(DIRS):

            @pl.when(present(da, db))
            def _():
                copy(d).wait_send()

    pl.run_scoped(
        body,
        pltpu.ACC(0)((16, 256), F32),
        pltpu.ACC(1)((16, 256), F32),
        pltpu.ACC(0)((16, 256), F32),
        pltpu.ACC(1)((16, 256), F32),
        pltpu.ACC(0)((GROUPS * 16, 256), F32),
        pltpu.ACC(1)((GROUPS * 16, 256), F32),
    )


def send_call(coords, weights, live):
    far = pl.BlockSpec(memory_space=pltpu.HBM)
    return pl.pallas_call(
        send_kernel,
        out_shape=(
            jax.ShapeDtypeStruct((GROUPS + 8, 128), jnp.int32),
            jax.ShapeDtypeStruct((DUMMY + 1, 8, 128), F32),
            jax.ShapeDtypeStruct((4, GROUPS, 8, 128), F32),
        ),
        in_specs=[far] * 3,
        out_specs=[pl.BlockSpec(memory_space=pltpu.VMEM)] * 3,
        scratch_shapes=[
            pltpu.VMEM((3, 1, 1, PART_DEV), jnp.int32),
            pltpu.VMEM((1, 1, PART_DEV), BF16),
            pltpu.VMEM((1, 1), jnp.int32),
            pltpu.VMEM((9, 4, PART_DEV), F32),
            pltpu.VMEM((8, 4, PART_DEV), F32),
            pltpu.SemaphoreType.DMA((3,)),
            pltpu.SemaphoreType.DMA((8,)),
            pltpu.SemaphoreType.DMA((8,)),
        ],
        compiler_params=pltpu.CompilerParams(collective_id=0, has_side_effects=True, vmem_limit_bytes=12 << 20),
    )(*[pltpu.with_memory_space_constraint(v, pltpu.HBM) for v in (coords, weights)], live)


LOG_SCALE = (S_BINS / 4.0) / math.log2(10.0)
LOG_BASE = -4.515457845
LEVELS_U = 24
LEVELS_V = 25
V_ROWS = 208
BINS = (2, TILES, 16, 128)
ENGINE = (
    ((2, 256, 128 * TILES), BF16),
    ((2, V_ROWS, 128 * TILES), BF16),
    (BINS, BF16),
    (BINS, BF16),
    (BINS, BF16),
    ((2, 2, 16, 128), BF16),
)


def engine(table_sm, rows_ref, own_ref, hot_u, hot_v, bin_u, bin_v, far_w, own_w):
    zero = jnp.zeros((16, 128), BF16)
    for half in range(2):
        hot_u[half, 8 * LEVELS_U :, :] = jnp.zeros((256 - 8 * LEVELS_U, 128 * TILES), BF16)

    def index(state, advance):
        for half in range(2):
            for mxu in range(2):
                g, b = state[0], state[1]
                group = jnp.minimum(g, GROUPS - 1)
                xi, yi, zi, wi = own_ref[0, group], own_ref[1, group], own_ref[2, group], own_ref[3, group]
                own_w[half, mxu] = jnp.concatenate([wi, wi], axis=0).astype(BF16)
                pair = table_sm[g, b]
                for t, row in ((2 * mxu, pair & 511), (2 * mxu + 1, pair >> 9)):
                    dx = xi - rows_ref[row, 0:1, :]
                    dy = yi - rows_ref[row, 1:2, :]
                    dz = zi - rows_ref[row, 2:3, :]
                    far_w[half, t] = jnp.broadcast_to(rows_ref[row, 3:4, :].astype(BF16), (16, 128))
                    dx2 = dx * dx
                    q = dx2 + dy * dy + dz * dz
                    s = jnp.floor(jnp.log2(q + 0.48) * LOG_SCALE + LOG_BASE)
                    near = jnp.floor(jnp.abs(dx) * lax.rsqrt(q) * float(MU_BINS) + 0.5)
                    mu = jnp.where(near * near * q > dx2 * float(MU_BINS * MU_BINS), near - 1.0, near)
                    c = s * float(MU_BINS) + jnp.minimum(mu, MU_BINS - 1.0)
                    u = jnp.floor(c * (1.0 / LEVELS_V) + 0.01)
                    v = c - u * float(LEVELS_V)
                    bin_u[half, t] = jnp.concatenate([u, u - 1.0], axis=0).astype(BF16)
                    bin_v[half, t] = jnp.concatenate([v, v - 1.0], axis=0).astype(BF16)
                state = advance(*state)
        return state

    def fill(half):
        for t in range(TILES):
            u2, v2, w_far, w_own = bin_u[half, t], bin_v[half, t], far_w[half, t], own_w[half, t // 2]
            lanes = slice(128 * t, 128 * t + 128)
            for k in range(LEVELS_U // 2):
                hot_u[half, 16 * k : 16 * k + 16, lanes] = jnp.where(u2 == jnp.bfloat16(2 * k), w_far, zero)
            for k in range(V_ROWS // 16):
                hot_v[half, 16 * k : 16 * k + 16, lanes] = jnp.where(v2 == jnp.bfloat16(2 * k), w_own, zero)

    def push(half):
        for mxu in range(2):
            pltpu.matmul_push_rhs(hot_u[half, :, 256 * mxu : 256 * mxu + 256], staging_register=half, mxu_index=mxu, transpose=True)

    def multiply(half, accs):
        for mxu in range(2):
            pltpu.matmul_acc_lhs(accs[mxu], hot_v[half, :, 256 * mxu : 256 * mxu + 256], load_staged_rhs=half)

    def run(state, advance, trips, sets, drain):
        state = index(state, advance)
        for half in range(2):
            fill(half)
            push(half)
        state = index(state, advance)
        for r in range(SUBREGIONS):

            def trip(_, state):
                for half in range(2):
                    multiply(half, sets[r % 2])
                for half in range(2):
                    fill(half)
                    push(half)
                return index(state, advance)

            state = lax.fori_loop(0, trips(r), trip, state)
            if r > 0:
                drain(r - 1, sets[(r - 1) % 2])
        last = sets[(SUBREGIONS - 1) % 2]
        for half in range(2):
            multiply(half, last)
        drain(SUBREGIONS - 1, last)

    return run


def count_kernel(table_ref, rows_ref, own_ref, out_ref, table_sm, sem):
    def body(a0, a1, b0, b1, *buffers):
        copy = pltpu.make_async_copy(table_ref, table_sm, sem)
        copy.start()
        for acc in (a0, a1, b0, b1):
            pltpu.matmul_pop(acc)
        run = engine(table_sm, rows_ref, own_ref, *buffers)
        copy.wait()

        def advance(g, b, left, region):
            over = b + 1 >= table_sm[g, 127]
            left = left - 1
            done = left <= 0
            region = jnp.where(done, jnp.minimum(region + 1, SUBREGIONS), region)
            b = jnp.where(done, table_sm[GROUPS + 3, region], jnp.where(over, 0, b + 1))
            g = jnp.where(done, table_sm[GROUPS + 2, region], jnp.where(over, g + 1, g))
            return g, b, jnp.where(done, 4 * table_sm[GROUPS + 1, region], left), region

        def drain(r, accs):
            out_ref[r] = pltpu.matmul_pop(accs[0]) + pltpu.matmul_pop(accs[1])

        state = (table_sm[GROUPS + 2, 0], table_sm[GROUPS + 3, 0], 4 * table_sm[GROUPS + 1, 0], jnp.int32(0))
        run(state, advance, lambda r: table_sm[GROUPS + 1, r], ((a0, a1), (b0, b1)), drain)

    pl.run_scoped(
        body,
        pltpu.ACC(0)((V_ROWS, 256), F32),
        pltpu.ACC(1)((V_ROWS, 256), F32),
        pltpu.ACC(0)((V_ROWS, 256), F32),
        pltpu.ACC(1)((V_ROWS, 256), F32),
        *(pltpu.VMEM(shape, dtype) for shape, dtype in ENGINE),
    )


def count_call(table, rows, own):
    vmem = pl.BlockSpec(memory_space=pltpu.VMEM)
    return pl.pallas_call(
        count_kernel,
        out_shape=jax.ShapeDtypeStruct((SUBREGIONS, V_ROWS, 256), F32),
        in_specs=[vmem, vmem, vmem],
        out_specs=vmem,
        scratch_shapes=[pltpu.SMEM((GROUPS + 8, 128), jnp.int32), pltpu.SemaphoreType.DMA],
        compiler_params=pltpu.CompilerParams(vmem_limit_bytes=6 << 20),
    )(table, rows, own)


def total_kernel(skies, counts_ref, table_ref, rows_ref, own_ref, packed_ref, total_ref, sum_ref, sent_ref, land_ref, table_sm, sem, send_sem, recv_sem):
    shell, sky = lax.axis_index("shell"), lax.axis_index("sky")
    barrier = pltpu.get_barrier_semaphore()
    load = pltpu.make_async_copy(table_ref, table_sm, sem)
    load.start()
    for k in range(1, skies):
        pl.semaphore_signal(barrier, inc=1, device_id=(shell, lax.rem(sky + k, skies)), device_id_type=MESH)

    def copy(k):
        return pltpu.make_async_remote_copy(
            src_ref=sent_ref,
            dst_ref=land_ref.at[k - 1],
            send_sem=send_sem.at[k - 1],
            recv_sem=recv_sem.at[k - 1],
            device_id=(shell, lax.rem(sky + k, skies)),
            device_id_type=MESH,
        )

    def body(a0, a1, b0, b1, small, large, *buffers):
        for acc in (a0, a1, b0, b1, small, large):
            pltpu.matmul_pop(acc)
        run = engine(table_sm, rows_ref, own_ref, *buffers)
        load.wait()

        def advance(g, b, left, region):
            over = b + 1 >= table_sm[g, 127]
            b = jnp.where(over, 0, b + 1)
            g = jnp.where(over, g + 1, g)
            g = jnp.where(g >= table_sm[GROUPS + 5, region], GROUPS, g)
            left = left - 1
            done = left <= 0
            region = jnp.where(done, jnp.minimum(region + 1, SUBREGIONS), region)
            g = jnp.where(done, table_sm[GROUPS + 4, region], g)
            return g, jnp.where(done, 0, b), jnp.where(done, 4 * EARLY, left), region

        def drain(r, accs):
            sum_ref[r] = counts_ref[r] + (pltpu.matmul_pop(accs[0]) + pltpu.matmul_pop(accs[1]))

        state = (table_sm[GROUPS + 4, 0], jnp.int32(0), jnp.int32(4 * EARLY), jnp.int32(0))
        run(state, advance, lambda r: EARLY, ((a0, a1), (b0, b1)), drain)

        lane_in = lax.broadcasted_iota(jnp.int32, (256, 256), 0) >> 3
        lane_out = lax.broadcasted_iota(jnp.int32, (256, 256), 1)
        diagonal = lax.broadcasted_iota(jnp.int32, (V_ROWS, 256), 0) & 7 == lax.broadcasted_iota(jnp.int32, (V_ROWS, 256), 1) & 7

        def folded(block):
            block = jnp.where(diagonal, block, 0.0).reshape(V_ROWS // 8, 8, 256)
            return jnp.concatenate([jnp.sum(block, axis=1), jnp.zeros((32 - V_ROWS // 8, 256), F32)], axis=0)

        def pack(blocks, acc):
            size = 8 * len(blocks)
            for k in range(4):
                rows = jnp.concatenate([block[8 * k : 8 * k + 8] for block in blocks], axis=0)
                high = rows.astype(BF16)
                rest = rows - high.astype(F32)
                middle = rest.astype(BF16)
                low = (rest - middle.astype(F32)).astype(BF16)
                parts = [high.astype(F32), middle.astype(F32), low.astype(F32)]
                if size == 8:
                    parts.append(jnp.zeros((8, 256), F32))
                pick = jnp.where(lane_in + 32 * k == lane_out, 1.0, 0.0).astype(BF16)
                pltpu.matmul_push_rhs(pick, staging_register=0, mxu_index=0)
                pltpu.matmul_acc_lhs(acc, jnp.concatenate(parts, axis=0).astype(BF16), load_staged_rhs=0)
            got = pltpu.matmul_pop(acc)
            return (got[0:size] + got[size : 2 * size] + got[2 * size : 3 * size])[:, 0:128]

        every = sum_ref[0]
        for r in range(1, SUBREGIONS):
            every = every + sum_ref[r]
        mine = pack([folded(every)], small)
        sent_ref[...] = mine
        pl.semaphore_wait(barrier, skies - 1)
        for k in range(1, skies):
            copy(k).start()
        packed_ref[...] = pack([folded(sum_ref[r]) for r in range(SUBREGIONS)], large)
        total = mine
        for k in range(1, skies):
            copy(k).wait_recv()
            total = total + land_ref[k - 1]
        total_ref[...] = total
        for k in range(1, skies):
            copy(k).wait_send()

    pl.run_scoped(
        body,
        pltpu.ACC(0)((V_ROWS, 256), F32),
        pltpu.ACC(1)((V_ROWS, 256), F32),
        pltpu.ACC(0)((V_ROWS, 256), F32),
        pltpu.ACC(1)((V_ROWS, 256), F32),
        pltpu.ACC(0)((32, 256), F32),
        pltpu.ACC(0)((24 * SUBREGIONS, 256), F32),
        *(pltpu.VMEM(shape, dtype) for shape, dtype in ENGINE),
    )


def total_call(counts, table, rows, own):
    skies = lax.axis_size("sky")
    vmem = pl.BlockSpec(memory_space=pltpu.VMEM)
    return pl.pallas_call(
        functools.partial(total_kernel, skies),
        out_shape=(jax.ShapeDtypeStruct((8 * SUBREGIONS, 128), F32), jax.ShapeDtypeStruct((8, 128), F32)),
        in_specs=[vmem] * 4,
        out_specs=(vmem, vmem),
        scratch_shapes=[
            pltpu.VMEM((SUBREGIONS, V_ROWS, 256), F32),
            pltpu.VMEM((8, 128), F32),
            pltpu.VMEM((skies - 1, 8, 128), F32),
            pltpu.SMEM((GROUPS + 8, 128), jnp.int32),
            pltpu.SemaphoreType.DMA,
            pltpu.SemaphoreType.DMA((skies - 1,)),
            pltpu.SemaphoreType.DMA((skies - 1,)),
        ],
        compiler_params=pltpu.CompilerParams(collective_id=1, has_side_effects=True, vmem_limit_bytes=10 << 20),
    )(counts, table, rows, own)


def edge_values():
    return [int(4.0 * 10.0 ** (4.0 * level / S_BINS) + 0.5) for level in range(S_BINS + 1)]


def bin_scale(patches):
    edges = edge_values()
    factor = SIDE_CELLS * SIDE_CELLS * SPAN_CELLS / (patches * PART_DEV * PART_DEV)
    values = []
    for level in range(S_BINS):
        volume = 4.0 * math.pi / 3.0 * (edges[level + 1] ** 1.5 - edges[level] ** 1.5) / MU_BINS
        values = values + [factor / volume] * MU_BINS
    return jnp.asarray(values, dtype=F32)


def unpacked(x):
    x = x.reshape(-1, 8, 4, 32).transpose(0, 3, 2, 1).reshape(-1, 32, 32)
    return x[:, :LEVELS_U, :LEVELS_V].reshape(-1, S_BINS * MU_BINS)


def local(coords, weights, live):
    tables = send_call(coords, weights, live)
    packed, total = total_call(count_call(*tables), *tables)
    leave = total[None] - packed.reshape(SUBREGIONS, 8, 128)
    return (unpacked(leave) * bin_scale(lax.axis_size("sky"))[None, :])[None]


def solution(mesh):
    in_specs = (P(None, "shell", "sky", None), P("shell", "sky", None), P("shell", "sky"))
    out_specs = P("shell", "sky", None)
    return jax.shard_map(local, mesh=mesh, in_specs=in_specs, out_specs=out_specs, check_vma=False)
```

profile of v0, /device:TPU:6, one launch (start us, length us, event | category | flops | bytes accessed | tf_op | source)
XLA Modules:
  0.0 38.2 jit_solution(17638636663030935835)
XLA Ops:
  0.7 12.1 %shard_map.46 = (s32[32,128]{1,0:T(8,128)S(1)}, f32[289,8,128]{2,1,0:T(8,128)S(1)}, f32[4,24,8,128]{3,2,1,0:T(8,128)S(1)}) custom-call(s32[3,1,1,512]{3,2,1,0:T(1,128)} %coords_hbm.1, bf16[1,1,512]{2,1,0:T(2,128)(2,1)} %weight_hbm.1, s32[1,1]{1,0:T(1,128)S(6)} %copy.13.live_hbm), custom_call_target="tpu_custom_call" | custom-call | tf_op jit(solution)/shard_map/pallas_call | solution.py:269
  12.7 4.3 %shard_map.47.counts_ref = f32[8,208,256]{2,1,0:T(8,128)S(1)} custom-call(s32[32,128]{1,0:T(8,128)S(1)} %get-tuple-element.10.table_ref, f32[289,8,128]{2,1,0:T(8,128)S(1)} %get-tuple-element.11.rows_ref, f32[4,24,8,128]{3,2,1,0:T(8,128)S(1)} %get-tuple-element.12.own_ref), custom_call_target="tpu_custom_call" | custom-call | tf_op jit(solution)/shard_map/pallas_call | solution.py:419
  17.1 0.0 copy-start
  17.1 20.0 %shard_map.48 = (f32[64,128]{1,0:T(8,128)S(1)}, f32[8,128]{1,0:T(8,128)S(1)}) custom-call(f32[8,208,256]{2,1,0:T(8,128)S(1)} %shard_map.47.counts_ref, s32[32,128]{1,0:T(8,128)S(1)} %get-tuple-element.10.table_ref, f32[289,8,128]{2,1,0:T(8,128)S(1)} %get-tuple-element.11.rows_ref, f32[4,24,8,128]{3,2,1,0:T(8,128)S(1)} %get-tuple-element.12.own_ref), custom_call_target="tpu_custom_call" | custom-call | tf_op jit(solution)/shard_map/pallas_call | solution.py:527
  37.1 0.1 sub.11
  37.2 0.1 reshape.46
  37.3 0.1 copy.9
  37.4 0.1 reshape.48
  37.5 0.0 copy-done
  37.5 0.6 %broadcast_multiply_fusion = f32[1,8,600]{2,1,0:T(8,128)} fusion(f32[1,8,600]{2,1,0:T(8,128)S(1)} %reshape.48, f32[600]{0:T(1024)S(1)} %copy-done), kind=kLoop, calls=%fused_computation.2 | loop fusion | flops 4800 | bytes 40800 | tf_op jit(solution)/shard_map/mul | solution.py:568
  (2 shorter events, 0.0 us)
Async XLA Ops:
  17.1 20.5 %copy-start = (f32[600]{0:T(1024)S(1)}, f32[600]{0:T(1024)}, u32[]{:S(2)}) copy-start(f32[600]{0:T(1024)} %constant.2.clone) | copy-start | bytes 7204
where the time goes:
time: 38.6 us; the launch traced here: 38.2 us
  Pallas kernels  36.4 us (94%)
  between operations  0.71 us (2%)
  other arithmetic  0.62 us (2%)
  local copies, waits for them, and re-layouts  0.42 us (1%)
    pallas_call x1, Pallas kernels, total_call(): pl.pallas_call(functools.partial(total_kernel, skies), out_shape=(jax.Sha...  20 us
    pallas_call x1, Pallas kernels, send_call(): pl.pallas_call(send_kernel, out_shape=(jax.ShapeDtypeStruct((GROUPS + 8,...  12.1 us
    pallas_call x1, Pallas kernels, count_call(): pl.pallas_call(count_kernel, out_shape=jax.ShapeDtypeStruct((SUBREGIONS,...  4.32 us

commit v1 on v0

--- a/solution.py
+++ b/solution.py
@@ -12,7 +12,7 @@
 S_BINS = 30
 MU_BINS = 20
 REACH = 199
-EARLY = 3
+EARLY = 4
 GROUPS = 24
 STEP = 16
 ROWS = PART_DEV // STEP
@@ -444,9 +444,13 @@
             device_id_type=MESH,
         )
 
-    def body(a0, a1, b0, b1, small, large, *buffers):
+    def body(a0, a1, b0, b1, small, large, pick_ref, *buffers):
         for acc in (a0, a1, b0, b1, small, large):
             pltpu.matmul_pop(acc)
+        lane_in = lax.broadcasted_iota(jnp.int32, (256, 256), 0) >> 3
+        lane_out = lax.broadcasted_iota(jnp.int32, (256, 256), 1)
+        for k in range(4):
+            pick_ref[k] = jnp.where(lane_in + 32 * k == lane_out, 1.0, 0.0).astype(BF16)
         run = engine(table_sm, rows_ref, own_ref, *buffers)
         load.wait()
 
@@ -467,8 +471,6 @@
         state = (table_sm[GROUPS + 4, 0], jnp.int32(0), jnp.int32(4 * EARLY), jnp.int32(0))
         run(state, advance, lambda r: EARLY, ((a0, a1), (b0, b1)), drain)
 
-        lane_in = lax.broadcasted_iota(jnp.int32, (256, 256), 0) >> 3
-        lane_out = lax.broadcasted_iota(jnp.int32, (256, 256), 1)
         diagonal = lax.broadcasted_iota(jnp.int32, (V_ROWS, 256), 0) & 7 == lax.broadcasted_iota(jnp.int32, (V_ROWS, 256), 1) & 7
 
         def folded(block):
@@ -486,8 +488,7 @@
                 parts = [high.astype(F32), middle.astype(F32), low.astype(F32)]
                 if size == 8:
                     parts.append(jnp.zeros((8, 256), F32))
-                pick = jnp.where(lane_in + 32 * k == lane_out, 1.0, 0.0).astype(BF16)
-                pltpu.matmul_push_rhs(pick, staging_register=0, mxu_index=0)
+                pltpu.matmul_push_rhs(pick_ref[k], staging_register=0, mxu_index=0)
                 pltpu.matmul_acc_lhs(acc, jnp.concatenate(parts, axis=0).astype(BF16), load_staged_rhs=0)
             got = pltpu.matmul_pop(acc)
             return (got[0:size] + got[size : 2 * size] + got[2 * size : 3 * size])[:, 0:128]
@@ -517,6 +518,7 @@
         pltpu.ACC(1)((V_ROWS, 256), F32),
         pltpu.ACC(0)((32, 256), F32),
         pltpu.ACC(0)((24 * SUBREGIONS, 256), F32),
+        pltpu.VMEM((4, 256, 256), BF16),
         *(pltpu.VMEM(shape, dtype) for shape, dtype in ENGINE),
     )
 

time: 38.6 us -> 38.4 us (level)
  the two profiles are of different devices: /device:TPU:6 before, /device:TPU:1 now
where the time goes in v1:
time: 38.4 us; the launch traced here: 39.1 us
  Pallas kernels  37.4 us (97%)
  between operations  0.71 us (2%)
  other arithmetic  0.62 us (2%)
  local copies, waits for them, and re-layouts  0.42 us (1%)
    pallas_call x1, Pallas kernels, total_call(): pl.pallas_call(functools.partial(total_kernel, skies), out_shape=(jax.Sha...  18.8 us
    pallas_call x1, Pallas kernels, send_call(): pl.pallas_call(send_kernel, out_shape=(jax.ShapeDtypeStruct((GROUPS + 8,...  12.6 us
    pallas_call x1, Pallas kernels, count_call(): pl.pallas_call(count_kernel, out_shape=jax.ShapeDtypeStruct((SUBREGIONS,...  6 us

profile of v1, /device:TPU:1, one launch (start us, length us, event | category | flops | bytes accessed | tf_op | source)
XLA Modules:
  0.0 39.1 jit_solution(14979883140973338698)
XLA Ops:
  0.7 12.6 %shard_map.46 = (s32[32,128]{1,0:T(8,128)S(1)}, f32[289,8,128]{2,1,0:T(8,128)S(1)}, f32[4,24,8,128]{3,2,1,0:T(8,128)S(1)}) custom-call(s32[3,1,1,512]{3,2,1,0:T(1,128)} %coords_hbm.1, bf16[1,1,512]{2,1,0:T(2,128)(2,1)} %weight_hbm.1, s32[1,1]{1,0:T(1,128)S(6)} %copy.13.live_hbm), custom_call_target="tpu_custom_call" | custom-call | tf_op jit(solution)/shard_map/pallas_call | solution.py:269
  13.2 6.0 %shard_map.47.counts_ref = f32[8,208,256]{2,1,0:T(8,128)S(1)} custom-call(s32[32,128]{1,0:T(8,128)S(1)} %get-tuple-element.10.table_ref, f32[289,8,128]{2,1,0:T(8,128)S(1)} %get-tuple-element.11.rows_ref, f32[4,24,8,128]{3,2,1,0:T(8,128)S(1)} %get-tuple-element.12.own_ref), custom_call_target="tpu_custom_call" | custom-call | tf_op jit(solution)/shard_map/pallas_call | solution.py:419
  19.3 0.0 copy-start
  19.3 18.8 %shard_map.48 = (f32[64,128]{1,0:T(8,128)S(1)}, f32[8,128]{1,0:T(8,128)S(1)}) custom-call(f32[8,208,256]{2,1,0:T(8,128)S(1)} %shard_map.47.counts_ref, s32[32,128]{1,0:T(8,128)S(1)} %get-tuple-element.10.table_ref, f32[289,8,128]{2,1,0:T(8,128)S(1)} %get-tuple-element.11.rows_ref, f32[4,24,8,128]{3,2,1,0:T(8,128)S(1)} %get-tuple-element.12.own_ref), custom_call_target="tpu_custom_call" | custom-call | tf_op jit(solution)/shard_map/pallas_call | solution.py:529
  38.0 0.1 sub.11
  38.1 0.1 reshape.46
  38.3 0.1 copy.9
  38.4 0.1 reshape.48
  38.5 0.0 copy-done
  38.5 0.6 %broadcast_multiply_fusion = f32[1,8,600]{2,1,0:T(8,128)} fusion(f32[1,8,600]{2,1,0:T(8,128)S(1)} %reshape.48, f32[600]{0:T(1024)S(1)} %copy-done), kind=kLoop, calls=%fused_computation.2 | loop fusion | flops 4800 | bytes 40800 | tf_op jit(solution)/shard_map/mul | solution.py:570
  (2 shorter events, 0.0 us)
Async XLA Ops:
  19.3 19.2 %copy-start = (f32[600]{0:T(1024)S(1)}, f32[600]{0:T(1024)}, u32[]{:S(2)}) copy-start(f32[600]{0:T(1024)} %constant.2.clone) | copy-start | bytes 7204
